TPU v7x, 32 devices: a whole 2x2x4 slice. The times are simulated.
32 devices in a mesh: ka: 2 (over x), band: 16 (over z, y, core).
Axes of the slice: x: 2, y: 2, z: 4, core: 2. Of those that a mesh axis runs over, the one named last changes fastest.
Arguments:
- psi_hat: float32 [2, 12, 2, 128, 128, 128], P('ka', None, None, 'band'), may hold values from -1.5 to 1.5
- occupations: int32 [2, 12], P('ka'), may hold values from 0 to 2
- weights: int32 [2], P('ka'), may hold values from 1 to 6
- density_in: float32 [128, 128, 128], P('band'), may hold values from -12 to 12
- dens_hist: float32 [8, 128, 128, 128], P(None, 'band'), may hold values from -3 to 3
- resid_hist: float32 [8, 128, 128, 128], P(None, 'band'), may hold values from -12 to 12
Outputs:
- out_density: float32 [128, 128, 128], P('band')
- mixed_density: float32 [128, 128, 128], P('band')
All inputs are finite; a program needn't handle non-finite values.
Results may differ from a plain program's by a relative error of at most 0.0003.
Values sent between devices are 32-bit elements; how exact they have to be, the bound alone decides.
A program may use at most 128 MiB of HBM per device.

v0:
```python
from functools import partial

import jax
import jax.numpy as jnp
from jax import lax
from jax.sharding import PartitionSpec as P

NG = 128


highest = lax.Precision.HIGHEST
beta_mix = 0.3
regular = 0.01


def dft_tables():
    indices = jnp.arange(NG, dtype=jnp.int32)
    product = indices[:, None] * indices[None, :] % NG
    angles = product.astype(jnp.float32) * jnp.float32(2.0 * 3.141592653589793 / NG)
    return (jnp.cos(angles), jnp.sin(angles))


def rotate(pattern, real_part, imag_part, cosine_table, sine_table):
    einsum = partial(jnp.einsum, precision=highest)
    out_real = einsum(pattern, real_part, cosine_table) - einsum(pattern, imag_part, sine_table)
    out_imag = einsum(pattern, real_part, sine_table) + einsum(pattern, imag_part, cosine_table)
    return (out_real, out_imag)


def history_gram(resid_hist):
    return jnp.einsum("hzxy,gzxy->hg", resid_hist, resid_hist, precision=highest)


def local_sums(residual_now, resid_hist):
    projections = jnp.einsum("hzxy,zxy->h", resid_hist, residual_now, precision=highest)[:, None]
    return jnp.concatenate([history_gram(resid_hist), projections], axis=1)


def finish_mix(density, base_density, dens_hist, resid_hist, summed):
    gram = summed[:, :-1]
    projections = summed[:, -1]
    system = gram + regular * jnp.diag(jnp.diag(gram))
    chol_factor = jnp.linalg.cholesky(system)
    mix_coefs = jax.scipy.linalg.cho_solve((chol_factor, True), projections)
    update = jnp.einsum(
        "h,hzxy->zxy", mix_coefs, dens_hist + beta_mix * resid_hist, precision=highest
    )
    return base_density + beta_mix * (density - base_density) - update


def shards(psi_hat, occupations, weights, density_in, dens_hist, resid_hist):
    cosine_table, sine_table = dft_tables()
    weight_total = lax.psum(jnp.sum(weights.astype(jnp.float32)), "ka")
    after_kz = rotate("bpqk,kz->bzpq", psi_hat[0, :, 0], psi_hat[0, :, 1], cosine_table, sine_table)
    after_ky = rotate("bzpq,qy->bzpy", after_kz[0], after_kz[1], cosine_table, sine_table)
    stacked = jnp.stack(after_ky, axis=1)
    received = lax.all_to_all(stacked, "band", split_axis=2, concat_axis=3, tiled=True)
    real_part, imag_part = rotate(
        "bzpy,px->bzxy", received[:, 0], received[:, 1], cosine_table, sine_table
    )
    power = (real_part * real_part + imag_part * imag_part) * jnp.float32(1.0 / NG**3)
    occ_float = occupations[0].astype(jnp.float32)
    pool_term = jnp.einsum("b,bzxy->zxy", occ_float, power, precision=highest)
    pool_term = pool_term * (weights[0].astype(jnp.float32) / weight_total)
    share = lax.psum_scatter(pool_term, "ka", scatter_dimension=1, tiled=True)
    share_width = share.shape[1]
    share_start = lax.axis_index("ka") * share_width
    base_density = lax.dynamic_slice_in_dim(density_in, share_start, share_width, 1)
    dens_part = lax.dynamic_slice_in_dim(dens_hist, share_start, share_width, 2)
    resid_part = lax.dynamic_slice_in_dim(resid_hist, share_start, share_width, 2)
    partial_terms = local_sums(share - base_density, resid_part)
    summed = lax.psum(partial_terms, ("ka", "band"))
    mixed_share = finish_mix(share, base_density, dens_part, resid_part, summed)
    density, mixed_density = (
        lax.all_gather(share, "ka", axis=1, tiled=True),
        lax.all_gather(mixed_share, "ka", axis=1, tiled=True),
    )
    return (density, mixed_density)


def solution(mesh):
    return jax.shard_map(
        shards,
        mesh=mesh,
        in_specs=(
            P("ka", None, None, "band", None, None),
            P("ka", None),
            P("ka"),
            P("band", None, None),
            P(None, "band", None, None),
            P(None, "band", None, None),
        ),
        out_specs=(P("band", None, None), P("band", None, None)),
        check_vma=False,
    )
```

profile of v0, /device:TPU:0, one launch (start us, length us, event | category | flops | bytes accessed | tf_op | source)
XLA Modules:
  0.0 529.3 jit_solution(17351105606221677500)
XLA Ops:
  7.2 8.3 %fusion.2 = f32[128,12,8,128]{3,0,2,1:T(8,128)S(1)} fusion(f32[1,12,2,8,128,128]{5,4,3,2,1,0:T(8,128)} %param.6), kind=kOutput, calls=%fused_computation.7 | convolution fusion | flops 2416148480 | bytes 12582912 | tf_op jit(solution)/shard_map/bpqk,kz->bzpq/dot_general | solution.py:26
  15.5 6.2 %fusion.6 = f32[128,12,8,128]{3,0,2,1:T(8,128)S(1)} fusion(f32[1,12,2,8,128,128]{5,4,3,2,1,0:T(8,128)S(1)} %copy-done.1), kind=kOutput, calls=%fused_computation.11 | convolution fusion | flops 2416148480 | bytes 12582912 | tf_op jit(solution)/shard_map/bpqk,kz->bzpq/dot_general | solution.py:26
  21.7 8.3 %fusion.4 = f32[128,12,8,128]{3,0,2,1:T(8,128)S(1)} fusion(f32[1,12,2,8,128,128]{5,4,3,2,1,0:T(8,128)} %param.6), kind=kOutput, calls=%fused_computation.9 | convolution fusion | flops 2416148480 | bytes 12582912 | tf_op jit(solution)/shard_map/bpqk,kz->bzpq/dot_general | solution.py:25
  30.0 8.1 %fusion.8 = f32[128,12,8,128]{3,0,2,1:T(8,128)S(1)} fusion(f32[1,12,2,8,128,128]{5,4,3,2,1,0:T(8,128)} %param.6), kind=kOutput, calls=%fused_computation.13 | convolution fusion | flops 2416148480 | bytes 12582912 | tf_op jit(solution)/shard_map/bpqk,kz->bzpq/dot_general | solution.py:25
  38.1 7.4 %fusion.10 = f32[12,128,8,128]{3,1,2,0:T(8,128)} fusion(f32[128,12,8,128]{3,0,2,1:T(8,128)S(1)} %fusion.6, f32[128,12,8,128]{3,0,2,1:T(8,128)S(1)} %fusion.2), kind=kOutput, calls=%fused_computation.15 | convolution fusion | flops 2417721344 | bytes 18874368 | tf_op jit(solution)/shard_map/bzpq,qy->bzpy/dot_general | solution.py:26
  45.5 7.7 %fusion.12 = f32[12,128,8,128]{3,1,2,0:T(8,128)} fusion(f32[128,12,8,128]{3,0,2,1:T(8,128)S(1)} %fusion.6, f32[128,12,8,128]{3,0,2,1:T(8,128)S(1)} %fusion.2), kind=kOutput, calls=%fused_computation.17 | convolution fusion | flops 2417721344 | bytes 18874368 | tf_op jit(solution)/shard_map/bzpq,qy->bzpy/dot_general | solution.py:25
  53.2 8.2 %add_bitcast_fusion = f32[12,1,128,8,128]{4,2,3,0,1:T(8,128)S(1)} fusion(f32[12,128,8,128]{3,1,2,0:T(8,128)} %fusion.10, f32[128,12,8,128]{3,0,2,1:T(8,128)S(1)} %fusion.8, f32[128,12,8,128]{3,0,2,1:T(8,128)S(1)} %fusion.4), kind=kOutput, calls=%fused_computation.24 | convolution fusion | flops 2419294208 | bytes 25165824 | tf_op jit(solution)/shard_map/bzpq,qy->bzpy/dot_general | solution.py:26
  61.4 7.9 %subtract_bitcast_fusion = f32[12,1,128,8,128]{4,2,3,0,1:T(8,128)} fusion(f32[12,128,8,128]{3,1,2,0:T(8,128)S(1)} %copy-done.2, f32[128,12,8,128]{3,0,2,1:T(8,128)S(1)} %fusion.8, f32[128,12,8,128]{3,0,2,1:T(8,128)S(1)} %fusion.4), kind=kOutput, calls=%fused_computation.25 | convolution fusion | flops 2419294208 | bytes 25165824 | tf_op jit(solution)/shard_map/bzpq,qy->bzpy/dot_general | solution.py:25
  69.3 9.0 %pad_maximum_fusion = f32[12,2,128,8,128]{4,2,3,0,1:T(8,128)} fusion(f32[12,1,128,8,128]{4,2,3,0,1:T(8,128)S(1)} %add_bitcast_fusion, f32[12,1,128,8,128]{4,2,3,0,1:T(8,128)} %subtract_bitcast_fusion), kind=kLoop, calls=%fused_computation.1 | loop fusion | flops 3145728 | bytes 25165824 | tf_op jit(solution)/shard_map/stack | solution.py:56
  78.3 16.3 %copy.60 = f32[12,2,128,8,128]{4,3,0,1,2:T(8,128)} copy(f32[12,2,128,8,128]{4,2,3,0,1:T(8,128)} %pad_maximum_fusion) | data formatting | bytes 25165824 | tf_op jit(solution)/shard_map/stack | solution.py:56
  94.6 7.5 %all-to-all-start = ((f32[12,2,128,8,128]{4,3,0,1,2:T(8,128)}), f32[12,2,128,8,128]{4,3,0,1,2:T(8,128)}, u32[]{:S(2)}, u32[]{:S(2)}) async-start(f32[12,2,128,8,128]{4,3,0,1,2:T(8,128)} %copy.60), calls=%async_computation | async-start | bytes 25165824 | tf_op jit(solution)/shard_map/all_to_all | solution.py:57
  102.8 6.1 %psum.14 = f32[]{:T(128)} all-reduce(f32[]{:T(128)} %bitcast.28), channel_id=1, replica_groups=mesh['ka'=2,'band'=16] {'ka'}, use_global_device_ids=true, to_apply=%region_0.1 | all-reduce | flops 1 | bytes 8 | tf_op jit(solution)/shard_map/psum | solution.py:53
  109.6 216.1 %all-to-all-done = f32[12,2,128,8,128]{4,3,0,1,2:T(8,128)} async-done(((f32[12,2,128,8,128]{4,3,0,1,2:T(8,128)}), f32[12,2,128,8,128]{4,3,0,1,2:T(8,128)}, u32[]{:S(2)}, u32[]{:S(2)}) %all-to-all-start) | async-done | bytes 12582944 | tf_op jit(solution)/shard_map/all_to_all | solution.py:57
  325.7 10.8 %copy.121 = f32[12,2,8,16,8,128]{5,4,3,2,1,0:T(8,128)} copy(f32[12,2,8,16,8,128]{5,4,0,1,2,3:T(8,128)} %bitcast.18) | data formatting | bytes 25165824 | tf_op jit(solution)/shard_map/all_to_all | solution.py:57
  336.5 10.0 %fusion.18 = f32[128,12,8,128]{3,0,2,1:T(8,128)} fusion(f32[12,2,8,128,128]{4,3,2,1,0:T(8,128)} %bitcast.136), kind=kOutput, calls=%fused_computation.26 | convolution fusion | flops 2416148480 | bytes 12582912 | tf_op jit(solution)/shard_map/bzpy,px->bzxy/dot_general | solution.py:26
  346.5 7.8 %fusion.19 = f32[128,12,8,128]{3,0,2,1:T(8,128)} fusion(f32[12,2,8,128,128]{4,3,2,1,0:T(8,128)S(1)} %bitcast.137), kind=kOutput, calls=%fused_computation.27 | convolution fusion | flops 2416148480 | bytes 12582912 | tf_op jit(solution)/shard_map/bzpy,px->bzxy/dot_general | solution.py:25
  354.3 7.8 %fusion.20 = f32[128,12,8,128]{3,0,2,1:T(8,128)} fusion(f32[12,2,8,128,128]{4,3,2,1,0:T(8,128)S(1)} %bitcast.138), kind=kOutput, calls=%fused_computation.28 | convolution fusion | flops 2416148480 | bytes 12582912 | tf_op jit(solution)/shard_map/bzpy,px->bzxy/dot_general | solution.py:26
  362.1 11.7 %multiply_bitcast_fusion = f32[12,8,128,128]{3,2,1,0:T(8,128)S(1)} fusion(f32[128,12,8,128]{3,0,2,1:T(8,128)} %fusion.18, f32[128,12,8,128]{3,0,2,1:T(8,128)} %fusion.20, f32[128,12,8,128]{3,0,2,1:T(8,128)} %fusion.19, f32[12,2,8,128,128]{4,3,2,1,0:T(8,128)S(1)} %bitcast.139), kind=kOutput, calls=%fused_computation.23 | convolution fusion | flops 2425585664 | bytes 31457280 | tf_op jit(solution)/shard_map/bzpy,px->bzxy/dot_general | solution.py:25
  373.8 10.8 %fusion = f32[1,8,128,128]{3,0,2,1:T(1,128)S(1)} fusion(f32[12,8,128,128]{3,2,1,0:T(8,128)S(1)} %multiply_bitcast_fusion, s32[1,12]{1,0:T(1,128)S(1)} %copy-done.5), kind=kOutput, calls=%fused_computation.3 | convolution fusion | flops 18874380 | bytes 6815792 | tf_op jit(solution)/shard_map/b,bzxy->zxy/dot_general | solution.py:63
  395.4 53.6 %reduce-scatter.2.cloned.1.call-done = f32[8,64,128]{2,1,0:T(8,128)} async-done(((f32[8,128,128]{2,1,0:T(8,128)}), f32[8,64,128]{2,1,0:T(8,128)}) %reduce-scatter.2.cloned.1.call-update) | async-done | bytes 262160 | tf_op jit(solution)/shard_map/reduce_scatter | solution.py:65
  455.3 39.7 %psum.15 = f32[8,9]{0,1:T(8,128)S(1)} all-reduce(f32[8,9]{0,1:T(8,128)S(1)} %pad_maximum_fusion.1), channel_id=1, replica_groups=mesh['ka'=2,'band'=16] {'ka','band'}, use_global_device_ids=true, to_apply=%region_2.3 | all-reduce | flops 72 | bytes 576 | tf_op jit(solution)/shard_map/psum | solution.py:72
  498.9 5.7 %fusion.34 = f32[1,8,64,128]{3,0,2,1:T(1,128)S(1)} fusion(f32[8,1,1,1]{0,1,3,2:T(1,128)S(1)} %convolution_bitcast_fusion, f32[8,8,64,128]{3,2,1,0:T(8,128)} %constant_dynamic-slice_fusion, f32[8,8,64,128]{3,2,1,0:T(8,128)S(1)} %constant_dynamic-slice_fusion.1), kind=kOutput, calls=%fused_computation.39 | convolution fusion | flops 7340032 | bytes 4456480 | tf_op jit(solution)/shard_map/h,hzxy->zxy/dot_general | solution.py:45
  504.6 8.4 %all_gather.7 = f32[8,128,128]{2,1,0:T(8,128)S(1)} all-gather(f32[8,64,128]{2,1,0:T(8,128)S(1)} %add_subtract_fusion), channel_id=1, replica_groups=mesh['ka'=2,'band'=16] {'ka'}, dimensions={1}, use_global_device_ids=true | all-gather | bytes 786432 | tf_op jit(solution)/shard_map/all_gather | solution.py:76
  513.1 7.3 %all_gather.6 = f32[8,128,128]{2,1,0:T(8,128)S(1)} all-gather(f32[8,64,128]{2,1,0:T(8,128)S(1)} %copy-done.3), channel_id=1, replica_groups=mesh['ka'=2,'band'=16] {'ka'}, dimensions={1}, use_global_device_ids=true | all-gather | bytes 786432 | tf_op jit(solution)/shard_map/all_gather | solution.py:75
  (39 shorter events, 22.6 us)
Async XLA Ops:
  7.2 8.3 %copy-start.1 = (f32[1,12,2,8,128,128]{5,4,3,2,1,0:T(8,128)S(1)}, f32[1,12,2,8,128,128]{5,4,3,2,1,0:T(8,128)}, u32[]{:S(2)}) copy-start(f32[1,12,2,8,128,128]{5,4,3,2,1,0:T(8,128)} %param.6) | copy-start | bytes 37748740
  53.2 8.2 %copy-start.2 = (f32[12,128,8,128]{3,1,2,0:T(8,128)S(1)}, f32[12,128,8,128]{3,1,2,0:T(8,128)}, u32[]{:S(2)}) copy-start(f32[12,128,8,128]{3,1,2,0:T(8,128)} %fusion.12) | copy-start | bytes 18874372
  94.6 231.1 %all-to-all-start = ((f32[12,2,128,8,128]{4,3,0,1,2:T(8,128)}), f32[12,2,128,8,128]{4,3,0,1,2:T(8,128)}, u32[]{:S(2)}, u32[]{:S(2)}) async-start(f32[12,2,128,8,128]{4,3,0,1,2:T(8,128)} %copy.60), calls=%async_computation | async-start | bytes 25165824 | tf_op jit(solution)/shard_map/all_to_all | solution.py:57
  102.1 346.9 %reduce-scatter.2.cloned.1.call-start = ((), (), s32[]{:S(2)}) async-start(), calls=%async_computation.2 | async-start | bytes 786432 | tf_op jit(solution)/shard_map/reduce_scatter | solution.py:65
  336.5 10.0 %copy-start = (f32[12,2,8,16,8,128]{5,4,3,2,1,0:T(8,128)S(1)}, f32[12,2,8,16,8,128]{5,4,3,2,1,0:T(8,128)}, u32[]{:S(2)}) copy-start(f32[12,2,8,16,8,128]{5,4,3,2,1,0:T(8,128)} %copy.121) | copy-start | bytes 37748740
  362.1 11.7 %copy-start.5 = (s32[1,12]{1,0:T(1,128)S(1)}, s32[1,12]{1,0:T(1,128)}, u32[]{:S(2)}) copy-start(s32[1,12]{1,0:T(1,128)} %param.7) | copy-start | bytes 148
  384.6 64.4 %copy-start.4 = (f32[8,128,128]{2,1,0:T(8,128)S(1)}, f32[8,128,128]{2,1,0:T(8,128)}, u32[]{:S(2)}) copy-start(f32[8,128,128]{2,1,0:T(8,128)} %param.9) | copy-start | bytes 1572868
  449.0 55.6 %copy-start.3 = (f32[8,64,128]{2,1,0:T(8,128)S(1)}, f32[8,64,128]{2,1,0:T(8,128)}, u32[]{:S(2)}) copy-start(f32[8,64,128]{2,1,0:T(8,128)} %reduce-scatter.2.cloned.1.call-done) | copy-start | bytes 786436
Sparse Core Ops, SparseCore 0:
  385.6 63.3 reduce-scatter.1
where the time goes:
time: 536 us; the launch traced here: 529 us
  waiting for transfers between devices  270 us (50%)
  matrix products  126 us (24%)
  blocking collectives  61.6 us (11%)
  local copies, waits for them, and re-layouts  34.6 us (6%)
  between operations  16 us (3%)
  other arithmetic  13.8 us (3%)
  starting transfers between devices  7.5 us (1%)
    all_to_all x1, waiting for transfers between devices, shards(): lax.all_to_all(stacked, 'band', split_axis=2, concat_axis=3, tiled=True)  216 us
    reduce_scatter x1, waiting for transfers between devices, shards(): share = lax.psum_scatter(pool_term, 'ka', scatter_dimension=1, tiled=True)  53.6 us
    psum x1, blocking collectives, shards(): summed = lax.psum(partial_terms, ('ka', 'band'))  39.7 us
    dot_general x3, matrix products, rotate(): einsum(pattern, imag_part, sine_table)  27.7 us
    dot_general x3, matrix products, rotate(): einsum(pattern, real_part, sine_table)  24.4 us
    dot_general x3, matrix products, rotate(): einsum(pattern, real_part, cosine_table)  23.8 us
    dot_general x3, matrix products, rotate(): einsum(pattern, imag_part, cosine_table)  23.4 us
    another operation x1, local copies, waits for them, and re-layouts, shards(): stacked = jnp.stack(after_ky, axis=1)  16.3 us
  transfers between devices with their start and end apart: 2, of which 2 were waited for; matrix products, arithmetic and copies ran while one was open for 2% of the time, Pallas kernels for 0%

commit v1 on v0

v1 whole, which is shorter than its diff:
```python
from functools import partial

import jax
import jax.numpy as jnp
import numpy as np
from jax import lax
from jax.experimental import pallas as pl
from jax.experimental.pallas import tpu as pltpu
from jax.sharding import PartitionSpec as P

highest = lax.Precision.HIGHEST
beta_mix = 0.3
regular = 0.01
CHUNKS = 3


def rotation_tables(size):
    indices = np.arange(size)
    angles = (indices[:, None] * indices[None, :] % size) * (2.0 * np.pi / size)
    cosine, sine = np.cos(angles), np.sin(angles)
    table = np.block([[cosine, sine], [-sine, cosine]]).astype(np.float32)
    high = table.astype(jnp.bfloat16)
    low = (table - high.astype(np.float32)).astype(jnp.bfloat16)
    return high, low


def split(value):
    high = value.astype(jnp.bfloat16)
    return high, (value - high.astype(jnp.float32)).astype(jnp.bfloat16)


def dot3(left, right, contract):
    dims = (contract, ((), ()))
    dot = partial(lax.dot_general, dimension_numbers=dims, preferred_element_type=jnp.float32)
    return dot(left[0], right[0]) + (dot(left[0], right[1]) + dot(left[1], right[0]))


def planes_kernel(psi_ref, wh_ref, wl_ref, th_ref, tl_ref, out_ref):
    devices, _, _, depth, planes, size = out_ref.shape
    for p in range(planes):
        pair = jnp.concatenate([psi_ref[0, 0, 0, p], psi_ref[0, 0, 1, p]], axis=1)
        after_kz = dot3((th_ref[...], tl_ref[...]), split(pair), ((1,), (1,)))
        rows = jnp.concatenate([after_kz[:size], after_kz[size:]], axis=1)
        after_ky = dot3(split(rows), (wh_ref[...], wl_ref[...]), ((1,), (0,)))
        for part in range(2):
            piece = after_ky[:, part * size : (part + 1) * size]
            out_ref[:, 0, part, :, p, :] = piece.reshape(devices, depth, size)


def power_kernel(scale_ref, recv_ref, th_ref, tl_ref, prev_ref, out_ref):
    devices, _, _, depth, planes, size = recv_ref.shape
    band = pl.program_id(0)
    factor = scale_ref[band]

    @pl.when(band == 0)
    def _():
        out_ref[...] = prev_ref[...]

    for z in range(0, depth, 2):
        columns = []
        for near in range(2):
            parts = [recv_ref[:, 0, c, z + near].reshape(devices * planes, size) for c in range(2)]
            columns.append(jnp.concatenate(parts, axis=0))
        field = dot3(
            (th_ref[...], tl_ref[...]), split(jnp.concatenate(columns, axis=1)), ((1,), (0,))
        )
        power = field[:size] * field[:size] + field[size:] * field[size:]
        for near in range(2):
            out_ref[z + near] += factor * power[:, near * size : (near + 1) * size]


def shards(psi_hat, occupations, weights, density_in, dens_hist, resid_hist):
    devices, points = lax.axis_size("band"), lax.axis_size("ka")
    _, bands, _, planes, size, _ = psi_hat.shape
    depth = size // devices
    chunks = CHUNKS if bands % CHUNKS == 0 else 1
    count = bands // chunks
    high, low = rotation_tables(size)
    wh, wl, th, tl = (jnp.asarray(t) for t in (high, low, high.T, low.T))

    weight = weights[0].astype(jnp.float32)
    share = weight / lax.psum(weight, "ka")
    factors = occupations[0].astype(jnp.float32) * (share * jnp.float32(1.0 / size**3))

    flops = 3 * 2 * count * planes * size * (2 * size) ** 2
    bytes_each = count * 2 * planes * size * size * 4
    whole = pl.BlockSpec((2 * size, 2 * size), lambda b: (0, 0))
    tile_spec = pl.BlockSpec((devices, 1, 2, depth, planes, size), lambda b: (0, b, 0, 0, 0, 0))
    slab = pl.BlockSpec((depth, size, size), lambda b: (0, 0, 0))
    limit = 40 * 1024 * 1024

    received = []
    for chunk in range(chunks):
        tiles = pl.pallas_call(
            planes_kernel,
            grid=(count,),
            in_specs=[
                pl.BlockSpec(
                    (1, 1, 2, planes, size, size),
                    lambda b, first=chunk * count: (0, first + b, 0, 0, 0, 0),
                ),
                whole, whole, whole, whole,
            ],
            out_specs=tile_spec,
            out_shape=jax.ShapeDtypeStruct(
                (devices, count, 2, depth, planes, size), jnp.float32
            ),
            compiler_params=pltpu.CompilerParams(vmem_limit_bytes=limit),
            cost_estimate=pl.CostEstimate(
                flops=2 * flops, bytes_accessed=2 * bytes_each, transcendentals=0
            ),
        )(psi_hat, wh, wl, th, tl)
        received.append(lax.all_to_all(tiles, "band", split_axis=0, concat_axis=0, tiled=True))

    gram = jnp.einsum("hzxy,gzxy->hg", resid_hist, resid_hist, precision=highest)
    start = jnp.einsum("hzxy,zxy->h", resid_hist, density_in, precision=highest)
    early = lax.psum(jnp.concatenate([gram, start[:, None]], axis=1), ("ka", "band"))
    early = early * jnp.float32(1.0 / points)
    gram, start = early[:, :-1], early[:, -1]
    system = gram + regular * jnp.diag(jnp.diag(gram))
    chol_factor = jnp.linalg.cholesky(system)

    pool = jnp.zeros((depth, size, size), jnp.float32)
    for chunk in range(chunks):
        pool = pl.pallas_call(
            power_kernel,
            grid=(count,),
            in_specs=[
                pl.BlockSpec(memory_space=pltpu.SMEM), tile_spec, whole, whole, slab,
            ],
            out_specs=slab,
            out_shape=jax.ShapeDtypeStruct((depth, size, size), jnp.float32),
            compiler_params=pltpu.CompilerParams(vmem_limit_bytes=limit),
            cost_estimate=pl.CostEstimate(
                flops=flops, bytes_accessed=bytes_each, transcendentals=0
            ),
        )(factors[chunk * count : (chunk + 1) * count], received[chunk], th, tl, pool)

    if points == 2:
        density = pool + lax.ppermute(pool, "ka", [(0, 1), (1, 0)])
    else:
        density = lax.psum(pool, "ka")
    late = lax.psum(jnp.sum(resid_hist * pool, axis=(1, 2, 3)), ("ka", "band"))
    mix_coefs = jax.scipy.linalg.cho_solve((chol_factor, True), late - start)
    history = dens_hist + beta_mix * resid_hist
    update = jnp.sum(mix_coefs[:, None, None, None] * history, axis=0)
    mixed_density = density_in + beta_mix * (density - density_in) - update
    return (density, mixed_density)


def solution(mesh):
    return jax.shard_map(
        shards,
        mesh=mesh,
        in_specs=(
            P("ka", None, None, "band", None, None),
            P("ka", None),
            P("ka"),
            P("band", None, None),
            P(None, "band", None, None),
            P(None, "band", None, None),
        ),
        out_specs=(P("band", None, None), P("band", None, None)),
        check_vma=False,
    )
```

time: 536 us -> 379 us (0.71); the launches traced: 529 us -> 379 us
  waiting for transfers between devices: 270 us -> 153 us
  matrix products: 126 us -> 28.2 us
  Pallas kernels: 0 us -> 60.3 us
  starting transfers between devices: 7.5 us -> 48.6 us
  local copies, waits for them, and re-layouts: 34.6 us -> 10.5 us
  between operations: 16 us -> 2.22 us
  blocking collectives: 61.6 us -> 67.1 us
    dot_general x16 -> x2, matrix products: 126 us -> 28 us  [the longest x1 17.7 us: shards(): jnp.einsum('hzxy,gzxy->hg', resid_hist, resid_hist, precision=highest)]
    all_to_all x1 -> x3, waiting for transfers between devices: 216 us -> 153 us  [shards(): lax.all_to_all(tiles, 'band', split_axis=0, concat_axis=0, tiled=True)]
    pallas_call x0 -> x6, Pallas kernels: none -> 60.3 us  [the longest x3 46.7 us: shards(): pl.pallas_call(planes_kernel, grid=(count,), in_specs=[pl.BlockSpec((1, 1...]
    reduce_scatter x1 -> x0, waiting for transfers between devices: 53.6 us -> none  [shards(): share = lax.psum_scatter(pool_term, 'ka', scatter_dimension=1, tiled=True)]
    all_to_all x1 -> x3, starting transfers between devices: 7.46 us -> 47.1 us  [shards(): lax.all_to_all(tiles, 'band', split_axis=0, concat_axis=0, tiled=True)]
    psum x2, blocking collectives: 45.8 us -> 67.1 us  [the longest x1 60.8 us: shards(): lax.psum(jnp.concatenate([gram, start[:, None]], axis=1), ('ka', 'band'))]
    another operation x3 -> x2, local copies, waits for them, and re-layouts: 16.5 us -> 0.14 us  [the longest x1 0.07 us: shards(): chol_factor = jnp.linalg.cholesky(system)]
    all_gather x2 -> x0, blocking collectives: 15.8 us -> none  [the longest x1 8.44 us: shards(): lax.all_gather(mixed_share, 'ka', axis=1, tiled=True)]
  transfers between devices with their start and end apart: 2 -> 4, of which waited for: 2 -> 3; matrix products, arithmetic and copies ran while one was open for 2% -> 10% of each run, Pallas kernels for 0% -> 11%
where the time goes in v1:
time: 379 us
  waiting for transfers between devices  153 us (40%)
  blocking collectives  67.1 us (18%)
  Pallas kernels  60.3 us (16%)
  starting transfers between devices  48.6 us (13%)
  matrix products  28.2 us (7%)
  local copies, waits for them, and re-layouts  10.5 us (3%)
  other arithmetic  9.07 us (2%)
    all_to_all x3, waiting for transfers between devices, shards(): lax.all_to_all(tiles, 'band', split_axis=0, concat_axis=0, tiled=True)  153 us
    psum x1, blocking collectives, shards(): lax.psum(jnp.concatenate([gram, start[:, None]], axis=1), ('ka', 'band'))  60.8 us
    all_to_all x3, starting transfers between devices, shards(): lax.all_to_all(tiles, 'band', split_axis=0, concat_axis=0, tiled=True)  47.1 us
    pallas_call x3, Pallas kernels, shards(): pl.pallas_call(planes_kernel, grid=(count,), in_specs=[pl.BlockSpec((1, 1...  46.7 us
    dot_general x1, matrix products, shards(): jnp.einsum('hzxy,gzxy->hg', resid_hist, resid_hist, precision=highest)  17.7 us
    pallas_call x3, Pallas kernels, shards(): pl.pallas_call(power_kernel, grid=(count,), in_specs=[pl.BlockSpec(memory...  13.6 us
    dot_general x1, matrix products, shards(): start = jnp.einsum('hzxy,zxy->h', resid_hist, density_in, precision=highest)  10.3 us
    unnamed x30, local copies, waits for them, and re-layouts  9.53 us
  transfers between devices with their start and end apart: 4, of which 3 were waited for; matrix products, arithmetic and copies ran while one was open for 10% of the time, Pallas kernels for 11%

profile of v1, /device:TPU:0, one launch (start us, length us, event | category | flops | bytes accessed | tf_op | source)
XLA Modules:
  0.0 378.7 jit_solution(14751098548045343650)
XLA Ops:
  1.5 0.9 copy-done.5
  2.4 0.9 copy-done.7
  4.3 15.6 %shard_map.115 = f32[16,4,2,8,8,128]{5,4,3,2,1,0:T(8,128)S(1)} custom-call(f32[1,12,2,8,128,128]{5,4,3,2,1,0:T(8,128)} %psi_ref.5, bf16[256,256]{1,0:T(8,128)(2,1)S(1)} %copy-done.7, bf16[256,256]{1,0:T(8,128)(2,1)S(1)} %copy-done.9, bf16[256,256]{1,0:T(8,128)(2,1)S(1)} %copy-done.3, bf16[256,256]{1,0:T(8,128)(2,1)S(1)} %copy-done.5), custom_call_target="tpu_custom_call" | custom-call | flops 3221225472 | bytes 8388608 | tf_op jit(solution)/shard_map/pallas_call | solution.py:94
  19.8 2.0 copy-done.2
  21.8 7.6 %all-to-all-start.2 = ((f32[16,4,2,8,8,128]{5,4,3,2,1,0:T(8,128)}), f32[16,4,2,8,8,128]{5,4,3,2,1,0:T(8,128)}, u32[]{:S(2)}, u32[]{:S(2)}) async-start(f32[16,4,2,8,8,128]{5,4,3,2,1,0:T(8,128)} %copy-done.2), calls=%async_computation.2 | async-start | bytes 8388608 | tf_op jit(solution)/shard_map/all_to_all | solution.py:113
  29.5 15.6 %shard_map.114 = f32[16,4,2,8,8,128]{5,4,3,2,1,0:T(8,128)S(1)} custom-call(f32[1,12,2,8,128,128]{5,4,3,2,1,0:T(8,128)} %psi_ref.5, bf16[256,256]{1,0:T(8,128)(2,1)S(1)} %copy-done.8, bf16[256,256]{1,0:T(8,128)(2,1)S(1)} %copy-done.10, bf16[256,256]{1,0:T(8,128)(2,1)S(1)} %copy-done.4, bf16[256,256]{1,0:T(8,128)(2,1)S(1)} %copy-done.6), custom_call_target="tpu_custom_call" | custom-call | flops 3221225472 | bytes 8388608 | tf_op jit(solution)/shard_map/pallas_call | solution.py:94
  45.1 1.9 copy-done.1
  47.0 60.0 %all-to-all-done.2.recv_ref = f32[16,4,2,8,8,128]{5,4,3,2,1,0:T(8,128)} async-done(((f32[16,4,2,8,8,128]{5,4,3,2,1,0:T(8,128)}), f32[16,4,2,8,8,128]{5,4,3,2,1,0:T(8,128)}, u32[]{:S(2)}, u32[]{:S(2)}) %all-to-all-start.2) | async-done | bytes 4194336 | tf_op jit(solution)/shard_map/all_to_all | solution.py:113
  107.0 19.7 %all-to-all-start.1 = ((f32[16,4,2,8,8,128]{5,4,3,2,1,0:T(8,128)}), f32[16,4,2,8,8,128]{5,4,3,2,1,0:T(8,128)}, u32[]{:S(2)}, u32[]{:S(2)}) async-start(f32[16,4,2,8,8,128]{5,4,3,2,1,0:T(8,128)} %copy-done.1), calls=%async_computation.1 | async-start | bytes 8388608 | tf_op jit(solution)/shard_map/all_to_all | solution.py:113
  126.7 15.6 %shard_map.113 = f32[16,4,2,8,8,128]{5,4,3,2,1,0:T(8,128)S(1)} custom-call(f32[1,12,2,8,128,128]{5,4,3,2,1,0:T(8,128)} %psi_ref.5, bf16[256,256]{1,0:T(8,128)(2,1)S(1)} %copy-done.8, bf16[256,256]{1,0:T(8,128)(2,1)S(1)} %copy-done.10, bf16[256,256]{1,0:T(8,128)(2,1)S(1)} %copy-done.4, bf16[256,256]{1,0:T(8,128)(2,1)S(1)} %copy-done.6), custom_call_target="tpu_custom_call" | custom-call | flops 3221225472 | bytes 8388608 | tf_op jit(solution)/shard_map/pallas_call | solution.py:94
  142.3 2.0 copy-done
  144.2 60.0 %all-to-all-done.1.recv_ref = f32[16,4,2,8,8,128]{5,4,3,2,1,0:T(8,128)} async-done(((f32[16,4,2,8,8,128]{5,4,3,2,1,0:T(8,128)}), f32[16,4,2,8,8,128]{5,4,3,2,1,0:T(8,128)}, u32[]{:S(2)}, u32[]{:S(2)}) %all-to-all-start.1) | async-done | bytes 4194336 | tf_op jit(solution)/shard_map/all_to_all | solution.py:113
  204.2 19.8 %all-to-all-start = ((f32[16,4,2,8,8,128]{5,4,3,2,1,0:T(8,128)}), f32[16,4,2,8,8,128]{5,4,3,2,1,0:T(8,128)}, u32[]{:S(2)}, u32[]{:S(2)}) async-start(f32[16,4,2,8,8,128]{5,4,3,2,1,0:T(8,128)} %copy-done), calls=%async_computation | async-start | bytes 8388608 | tf_op jit(solution)/shard_map/all_to_all | solution.py:113
  224.7 6.3 %psum.21 = f32[]{:T(128)} all-reduce(f32[]{:T(128)} %bitcast), channel_id=1, replica_groups=mesh['ka'=2,'band'=16] {'ka'}, use_global_device_ids=true, to_apply=%region_0.0 | all-reduce | flops 1 | bytes 8 | tf_op jit(solution)/shard_map/psum | solution.py:82
  231.7 17.7 %fusion.4 = f32[8,8]{0,1:T(8,128)S(1)} fusion(f32[8,8,128,128]{3,2,1,0:T(8,128)} %param.15), kind=kOutput, calls=%fused_computation.7 | convolution fusion | flops 100663296 | bytes 4194560 | tf_op jit(solution)/shard_map/hzxy,gzxy->hg/dot_general | solution.py:115
  249.4 10.3 %fusion.7 = f32[8,1]{0,1:T(1,128)S(1)} fusion(f32[8,8,128,128]{3,2,1,0:T(8,128)S(1)} %copy-done.11, f32[8,128,128,1]{2,1,0,3:T(8,128)S(1)} %bitcast.46), kind=kOutput, calls=%fused_computation.8 | convolution fusion | flops 12582912 | bytes 4718624 | tf_op jit(solution)/shard_map/hzxy,zxy->h/dot_general | solution.py:116
  259.8 4.5 %shard_map.116.prev_ref = f32[8,128,128]{2,1,0:T(8,128)S(1)} custom-call(f32[4]{0:T(128)S(1)} %get-tuple-element.6.scale_ref, f32[16,4,2,8,8,128]{5,4,3,2,1,0:T(8,128)} %all-to-all-done.2.recv_ref, bf16[256,256]{1,0:T(8,128)(2,1)S(1)} %copy-done.4, bf16[256,256]{1,0:T(8,128)(2,1)S(1)} %copy-done.6, f32[8,128,128]{2,1,0:T(8,128)S(1)} %broadcast_in_dim.36.prev_ref), custom_call_target="tpu_custom_call" | custom-call | flops 1610612736 | bytes 4194304 | tf_op jit(solution)/shard_map/pallas_call | solution.py:125
  264.3 4.5 %shard_map.117.prev_ref = f32[8,128,128]{2,1,0:T(8,128)S(1)} custom-call(f32[4]{0:T(128)S(1)} %get-tuple-element.7.scale_ref, f32[16,4,2,8,8,128]{5,4,3,2,1,0:T(8,128)} %all-to-all-done.1.recv_ref, bf16[256,256]{1,0:T(8,128)(2,1)S(1)} %copy-done.4, bf16[256,256]{1,0:T(8,128)(2,1)S(1)} %copy-done.6, f32[8,128,128]{2,1,0:T(8,128)S(1)} %shard_map.116.prev_ref), custom_call_target="tpu_custom_call" | custom-call | flops 1610612736 | bytes 4194304 | tf_op jit(solution)/shard_map/pallas_call | solution.py:125
  268.8 32.8 %all-to-all-done.recv_ref = f32[16,4,2,8,8,128]{5,4,3,2,1,0:T(8,128)} async-done(((f32[16,4,2,8,8,128]{5,4,3,2,1,0:T(8,128)}), f32[16,4,2,8,8,128]{5,4,3,2,1,0:T(8,128)}, u32[]{:S(2)}, u32[]{:S(2)}) %all-to-all-start) | async-done | bytes 4194336 | tf_op jit(solution)/shard_map/all_to_all | solution.py:113
  301.6 4.6 %shard_map.118 = f32[8,128,128]{2,1,0:T(8,128)S(1)} custom-call(f32[4]{0:T(128)S(1)} %get-tuple-element.8.scale_ref, f32[16,4,2,8,8,128]{5,4,3,2,1,0:T(8,128)} %all-to-all-done.recv_ref, bf16[256,256]{1,0:T(8,128)(2,1)S(1)} %copy-done.4, bf16[256,256]{1,0:T(8,128)(2,1)S(1)} %copy-done.6, f32[8,128,128]{2,1,0:T(8,128)S(1)} %shard_map.117.prev_ref), custom_call_target="tpu_custom_call" | custom-call | flops 1610612736 | bytes 4194304 | tf_op jit(solution)/shard_map/pallas_call | solution.py:125
  306.8 1.5 collective-permute-start
  308.3 60.8 %all-reduce = (f32[8,9]{0,1:T(8,128)S(1)}, f32[8]{0:T(128)S(1)}) all-reduce(f32[8,9]{0,1:T(8,128)S(1)} %pad_maximum_fusion, f32[8]{0:T(128)S(1)} %multiply_reduce_fusion.1), channel_id=1, replica_groups=mesh['ka'=2,'band'=16] {'ka','band'}, use_global_device_ids=true, to_apply=%region_1.0 | all-reduce | flops 80 | bytes 640 | tf_op jit(solution)/shard_map/psum | solution.py:117
  373.1 4.6 %multiply_reduce_fusion = f32[8,128,128]{2,1,0:T(8,128)S(1)} fusion(f32[8,8,128,128]{3,2,1,0:T(8,128)} %param.14, f32[8,8,128,128]{3,2,1,0:T(8,128)} %param.15, f32[8]{0:T(128)S(1)} %convolution_bitcast_fusion), kind=kLoop, calls=%fused_computation.1 | loop fusion | flops 4063232 | bytes 8912928 | tf_op jit(solution)/shard_map/reduce_sum | solution.py:146
  377.6 1.1 add_subtract_fusion
  (47 shorter events, 6.5 us)
Async XLA Ops:
  0.6 0.9 copy-start.3
  1.5 0.9 copy-start.5
  2.4 0.9 copy-start.7
  3.3 0.9 copy-start.9
  19.8 2.0 copy-start.2
  21.8 7.6 %copy-start.4 = (bf16[256,256]{1,0:T(8,128)(2,1)S(1)}, bf16[256,256]{1,0:T(8,128)(2,1)}, u32[]{:S(2)}) copy-start(bf16[256,256]{1,0:T(8,128)(2,1)} %constant.78.clone.th_ref) | copy-start | bytes 393220
  21.8 7.6 %copy-start.6 = (bf16[256,256]{1,0:T(8,128)(2,1)S(1)}, bf16[256,256]{1,0:T(8,128)(2,1)}, u32[]{:S(2)}) copy-start(bf16[256,256]{1,0:T(8,128)(2,1)} %constant.79.clone.tl_ref) | copy-start | bytes 393220
  21.8 7.6 %copy-start.8 = (bf16[256,256]{1,0:T(8,128)(2,1)S(1)}, bf16[256,256]{1,0:T(8,128)(2,1)}, u32[]{:S(2)}) copy-start(bf16[256,256]{1,0:T(8,128)(2,1)} %constant.76.clone.wh_ref) | copy-start | bytes 393220
  21.8 7.7 %copy-start.10 = (bf16[256,256]{1,0:T(8,128)(2,1)S(1)}, bf16[256,256]{1,0:T(8,128)(2,1)}, u32[]{:S(2)}) copy-start(bf16[256,256]{1,0:T(8,128)(2,1)} %constant.77.clone.wl_ref) | copy-start | bytes 393220
  21.8 85.2 %all-to-all-start.2 = ((f32[16,4,2,8,8,128]{5,4,3,2,1,0:T(8,128)}), f32[16,4,2,8,8,128]{5,4,3,2,1,0:T(8,128)}, u32[]{:S(2)}, u32[]{:S(2)}) async-start(f32[16,4,2,8,8,128]{5,4,3,2,1,0:T(8,128)} %copy-done.2), calls=%async_computation.2 | async-start | bytes 8388608 | tf_op jit(solution)/shard_map/all_to_all | solution.py:113
  45.1 1.9 copy-start.1
  107.0 97.2 %all-to-all-start.1 = ((f32[16,4,2,8,8,128]{5,4,3,2,1,0:T(8,128)}), f32[16,4,2,8,8,128]{5,4,3,2,1,0:T(8,128)}, u32[]{:S(2)}, u32[]{:S(2)}) async-start(f32[16,4,2,8,8,128]{5,4,3,2,1,0:T(8,128)} %copy-done.1), calls=%async_computation.1 | async-start | bytes 8388608 | tf_op jit(solution)/shard_map/all_to_all | solution.py:113
  142.3 2.0 copy-start
  204.2 45.1 %copy-start.13 = (f32[8,128,128]{2,1,0:T(8,128)S(1)}, f32[8,128,128]{2,1,0:T(8,128)}, u32[]{:S(2)}) copy-start(f32[8,128,128]{2,1,0:T(8,128)} %param.13) | copy-start | bytes 1572868
  204.2 97.4 %all-to-all-start = ((f32[16,4,2,8,8,128]{5,4,3,2,1,0:T(8,128)}), f32[16,4,2,8,8,128]{5,4,3,2,1,0:T(8,128)}, u32[]{:S(2)}, u32[]{:S(2)}) async-start(f32[16,4,2,8,8,128]{5,4,3,2,1,0:T(8,128)} %copy-done), calls=%async_computation | async-start | bytes 8388608 | tf_op jit(solution)/shard_map/all_to_all | solution.py:113
  231.7 17.7 %copy-start.11 = (f32[8,8,128,128]{3,2,1,0:T(8,128)S(1)}, f32[8,8,128,128]{3,2,1,0:T(8,128)}, u32[]{:S(2)}) copy-start(f32[8,8,128,128]{3,2,1,0:T(8,128)} %param.15) | copy-start | bytes 12582916
  231.7 28.0 %copy-start.14 = (s32[1,12]{1,0:T(1,128)S(1)}, s32[1,12]{1,0:T(1,128)}, u32[]{:S(2)}) copy-start(s32[1,12]{1,0:T(1,128)} %param.11) | copy-start | bytes 148
  301.6 4.6 %copy-start.12 = (f32[8,8,128,128]{3,2,1,0:T(8,128)S(1)}, f32[8,8,128,128]{3,2,1,0:T(8,128)}, u32[]{:S(2)}) copy-start(f32[8,8,128,128]{3,2,1,0:T(8,128)} %param.15) | copy-start | bytes 12582916
  306.8 70.8 %collective-permute-start = (f32[8,128,128]{2,1,0:T(8,128)S(1)}, f32[8,128,128]{2,1,0:T(8,128)S(1)}, u32[]{:S(2)}, u32[]{:S(2)}) collective-permute-start(f32[8,128,128]{2,1,0:T(8,128)S(1)} %shard_map.118), channel_id=1, source_target_pairs={{0,16},{16,0},{1,17},{17,1},{2,18},{18,2},{3,19},{19,3},{4,20},{20... | collective-permute-start | bytes 1572872 | tf_op jit(solution)/shard_map/ppermute | solution.py:140
